TPU v7x, 128 devices: a whole 4x4x4 slice. The times are simulated.
128 devices in a mesh: gx: 8 (over y, z_hi), gy: 8 (over x, core), gz: 2 (over z_lo).
Axes of the slice: x: 4, y: 4, z: 4 (z_hi: 2, z_lo: 2; z = z_hi * 2 + z_lo), core: 2. Of those that a mesh axis runs over, the one named last changes fastest.
Arguments:
- density: float32 [32, 256, 256], P('gx', 'gy', 'gz'), may hold values from 0.6 to 1.4
- velocity: float32 [3, 32, 256, 256], P(None, 'gx', 'gy', 'gz'), may hold values from -0.3 to 0.3
- solid_mask: int32 [32, 256, 256], P('gx', 'gy', 'gz'), may hold values 0 or 1
Outputs:
- density_final: float32 [32, 256, 256], P('gx', 'gy', 'gz')
- momentum: float32 [3, 32, 256, 256], P(None, 'gx', 'gy', 'gz')
All inputs are finite; a program needn't handle non-finite values.
Results may differ from a plain program's by a relative error of at most 0.0003.
Values sent between devices are 32-bit elements.
No kernel may reach another device: no remote copies, remote signals or barrier semaphores. Data moves between devices by JAX's collectives and lax.ppermute only.
A program may use at most 64 MiB of HBM per device.

v0:
```python
import jax
import jax.numpy as jnp
from jax import lax
from jax.experimental import pallas as pl
from jax.experimental.pallas import tpu as pltpu
from jax.sharding import PartitionSpec as P


VELOCITIES = [
    (0, 0, 0),
    (1, 0, 0),
    (-1, 0, 0),
    (0, 1, 0),
    (0, -1, 0),
    (0, 0, 1),
    (0, 0, -1),
    (1, 1, 0),
    (-1, -1, 0),
    (1, -1, 0),
    (-1, 1, 0),
    (1, 0, 1),
    (-1, 0, -1),
    (1, 0, -1),
    (-1, 0, 1),
    (0, 1, 1),
    (0, -1, -1),
    (0, 1, -1),
    (0, -1, 1),
]
PAIRS = [(q, q + 1) for q in range(1, 19, 2)]
RELAX_RATE = 1.25
AXES = ("gx", "gy", "gz")
F32 = jnp.float32
VMEM = pl.BlockSpec(memory_space=pltpu.VMEM)
MIB = 1 << 20
PACK_LIMIT = 66_600_000
INNER_FLOPS = 100_000_000


def lanes():
    return lax.broadcasted_iota(jnp.int32, (8, 128), 1)


def rows():
    return lax.broadcasted_iota(jnp.int32, (8, 128), 0)


def roll(v, shift, axis):
    shift %= v.shape[axis]
    return pltpu.roll(v, shift, axis) if shift else v


def permuted(x, target):
    pairs = []
    for gx in range(8):
        for gy in range(8):
            for gz in range(2):
                tx, ty, tz = target(gx, gy, gz)
                pairs.append(((gx * 8 + gy) * 2 + gz, ((tx % 8) * 8 + ty % 8) * 2 + tz % 2))
    return lax.ppermute(x, AXES, pairs)


def pack_kernel(d_hbm, v_hbm, m_hbm, block, rest, zcols, d, v, m, sems):
    odd = lax.axis_index("gx") % 2
    sign = (1 - 2 * odd).astype(F32)
    copies = [
        pltpu.make_async_copy(src, dst, sems.at[i])
        for i, (src, dst) in enumerate(((m_hbm, m), (v_hbm, v), (d_hbm, d)))
    ]
    for copy in copies:
        copy.start()
    for copy in copies:
        copy.wait()
    lane = lanes()
    packed = [jnp.zeros((8, 128), F32) for _ in range(5)]
    for plane in range(4):
        for t in range(4):
            at = pl.ds(8 * t, 8)
            src = plane + odd * (3 - 2 * plane)
            solid = m[src, at, :] == 1
            fields = [d[src, at, :]]
            fields += [jnp.where(solid, -v[i, src, at, :], v[i, src, at, :]) for i in range(3)]
            fields[1] = fields[1] * sign
            fields.append(jnp.where(solid, 1.0, 0.0).astype(F32))
            base = plane * 32 + t * 8
            inside = (lane >= base) & (lane < base + 8)
            for f in range(5):
                if f < 3:
                    block[f, plane, at, :] = fields[f]
                else:
                    rest[f - 3, plane, at, :] = fields[f]
                packed[f] = jnp.where(inside, roll(fields[f], base + 4, 1), packed[f])
    for f in range(5):
        zcols[8 * f : 8 * f + 8, :] = packed[f]


def second_message_kernel(rest, zrecv, out):
    for f in range(2):
        for plane in range(4):
            slab = (f * 4 + plane) * 32
            out[slab : slab + 32, :] = rest[f, plane]
    out[256:296, :] = zrecv[...]


def source(blocks, f, p, row, count):
    first, rest = blocks[(2, 0, 1)[p // 4]]
    plane = p - 4 if 4 <= p < 8 else (11 - p if p >= 8 else 3 - p)
    if f < 3:
        v = first[f, plane, row : row + count, :]
    elif 4 <= p < 8:
        v = rest[f - 3, plane, row : row + count, :]
    else:
        slab = ((f - 3) * 4 + plane) * 32
        v = rest[slab + row : slab + row + count, :]
    return -v if f == 1 and not 4 <= p < 8 else v


def zcolumns(blocks, zrecv, f, p):
    if 4 <= p < 8:
        return zrecv[8 * f : 8 * f + 8, :], (p - 4) * 32
    v = blocks[1 if p >= 8 else 2][1][256 + 8 * f : 264 + 8 * f, :]
    return (-v if f == 1 else v), ((11 - p) if p >= 8 else (3 - p)) * 32


def y_message_kernel(first_own, rest_own, zrecv, first_pair, rest_pair, to_core, to_chip):
    blocks = ((first_own, rest_own), (first_pair, rest_pair), None)
    first = lax.axis_index("gy") % 2 == 0
    lane = lanes()
    for f in range(5):
        for i in range(8):
            top = source(blocks, f, i + 4, 28, 4)
            bottom = source(blocks, f, i + 4, 0, 4)
            at = pl.ds((f * 8 + i) * 4, 4)
            to_core[at, :] = jnp.where(first, top, bottom)
            to_chip[at, :] = jnp.where(first, bottom, top)
        edge_low = jnp.zeros((8, 128), F32)
        edge_high = jnp.zeros((8, 128), F32)
        for i in range(8):
            z, base = zcolumns(blocks, zrecv, f, i + 4)
            inside = (lane >= i * 8) & (lane < i * 8 + 8)
            edge_low = jnp.where(inside, roll(z, i * 8 - base, 1), edge_low)
            edge_high = jnp.where(inside, roll(z, i * 8 - base - 24, 1), edge_high)
        edge_high = roll(edge_high, 4, 0)
        at = pl.ds(160 + f * 4, 4)
        to_core[at, :] = jnp.where(first, edge_high, edge_low)[:4]
        to_chip[at, :] = jnp.where(first, edge_low, edge_high)[:4]


def y_halo(from_core, from_chip, row):
    first = lax.axis_index("gy") % 2 == 0
    a, b = from_core[row : row + 4, :], from_chip[row : row + 4, :]
    return jnp.concatenate([jnp.where(first, a, b), jnp.where(first, b, a)], axis=0)


def halo_message_kernel(from_core, from_chip, _, out):
    for f in range(5):
        for i in range(4):
            at = (f * 4 + i) * 8
            out[at : at + 8, :] = y_halo(from_core, from_chip, (f * 8 + 4 + i) * 4)
        out[160 + 8 * f : 168 + 8 * f, :] = roll(y_halo(from_core, from_chip, 160 + f * 4), -32, 1)


def populations(weighted, base, h, rest):
    even, odd = [], []
    double = weighted + weighted
    base2 = base + base
    for q, _ in PAIRS:
        c = VELOCITIES[q]
        terms = [(h[i], c[i]) for i in range(3) if c[i]]
        k = terms[0][0]
        if len(terms) == 2:
            k = k + terms[1][0] if terms[1][1] > 0 else k - terms[1][0]
            m = weighted * k
            even.append(base + m * k)
        else:
            m = double * k
            even.append(base2 + m * k)
        odd.append(m)
    return rest * base, even, odd


def equilibrium(density, velocity):
    h = [1.5 * u for u in velocity]
    w = density * (1.0 / 36.0)
    square = h[0] * h[0] + h[1] * h[1] + h[2] * h[2]
    still, even, odd = populations(w + w, w - w * (square * (2.0 / 3.0)), h, 12.0)
    out = [still]
    for e, o in zip(even, odd):
        out += [e + o, e - o]
    return out


def momentum_of(diff):
    total = [None, None, None]
    for (q, _), d in zip(PAIRS, diff):
        for i in range(3):
            c = VELOCITIES[q][i]
            if c:
                total[i] = d if total[i] is None else total[i] + d if c > 0 else total[i] - d
    return total


def collide(f, mask):
    total = [f[a] + f[b] for a, b in PAIRS]
    diff = [f[a] - f[b] for a, b in PAIRS]
    r = f[0]
    for s in total:
        r = r + s
    j = momentum_of(diff)
    solid = mask > 0.5
    inverse = jnp.where(solid, 0.0, 1.5 / r)
    w = jnp.where(solid, 0.0, r * (RELAX_RATE / 36.0))
    h = [x * inverse for x in j]
    square = h[0] * h[0] + h[1] * h[1] + h[2] * h[2]
    still, even, odd = populations(w + w, w - w * (square * (2.0 / 3.0)), h, 12.0)
    a = jnp.where(solid, 0.5, 0.5 * (1.0 - RELAX_RATE))
    b = jnp.where(solid, -0.5, 0.5 * (1.0 - RELAX_RATE))
    out = [still + (a + a) * f[0]]
    for s, d, e, o in zip(total, diff, even, odd):
        p, m = a * s + e, b * d + o
        out += [p + m, p - m]
    return out


PLUS = [5, 11, 14, 15, 18]
MINUS = [6, 12, 13, 16, 17]


def streamed_column(hg, q, p, turn=0):
    cx, cy, cz = VELOCITIES[q]
    v = hg[p - cx, q]
    if not cy:
        return roll(v, cz + turn, 1)
    v = roll(v, cy, 0)
    edge = 0 if cy > 0 else 7
    return jnp.where(rows() == edge, roll(v, cz + turn + 8 * cy, 1), roll(v, cz + turn, 1))


def advance_columns(src, dst, hs, xs, inj, planes, tiles):
    inner = (lanes() & 7) >= 4
    for p in planes:
        f = [streamed_column(src, q, p) if dst is not None or q in PLUS else None for q in range(19)]
        for k in range(5):
            xs[p, k] = jnp.where(inner, f[PLUS[k]], streamed_column(src, MINUS[k], p, 64))
        if dst is not None:
            for q, v in enumerate(collide(f, hs[p, 4])):
                dst[p, q] = v
    for p in planes:
        for k in range(5):
            x = xs[p, k]
            for tile in tiles:
                inj[p, k, 8 * tile : 8 * tile + 8, :] = roll(x, -(tile * 8 + 4), 1)


def pulled(load, edge):
    lane = lanes()
    sides = [edge(k) for k in range(5)]
    out = []
    for q in range(19):
        cz = VELOCITIES[q][2]
        v = load(q)
        if cz > 0:
            v = jnp.where(lane == 0, sides[PLUS.index(q)], roll(v, 1, 1))
        elif cz < 0:
            v = jnp.where(lane == 127, sides[MINUS.index(q)], roll(v, 127, 1))
        out.append(v)
    return out


def main_pull(g, inj, p, t):
    def load(q):
        cx, cy, _ = VELOCITIES[q]
        return g[p - cx, q, 8 + 8 * t - cy : 16 + 8 * t - cy, :]

    return pulled(load, lambda k: inj[p, k, 8 + 8 * t : 16 + 8 * t, :])


def framed(ref, index, radius, shift=0):
    top = ref[index + (slice(8 - radius - shift, 16 - radius - shift), slice(None))]
    bottom = ref[index + (slice(32 + radius - shift, 40 + radius - shift), slice(None))]
    return jnp.where(rows() < 4, top, bottom)


def put_framed(ref, index, radius, v):
    ref[index + (slice(8 - radius, 12 - radius), slice(None))] = v[:4]
    ref[index + (slice(36 + radius, 40 + radius), slice(None))] = v[4:]


def frame_pull(g, inj, p, radius):
    def load(q):
        cx, cy, _ = VELOCITIES[q]
        return framed(g, (p - cx, q), radius, cy)

    return pulled(load, lambda k: framed(inj, (p, k), radius))


def moments(f):
    r = f[0]
    for a, b in PAIRS:
        r = r + (f[a] + f[b])
    return [r] + momentum_of([f[a] - f[b] for a, b in PAIRS])


def inner(blocks, zrecv, planes, s, hs, levels, columns_of, xs, inj, halo=None):
    lane = lanes()
    tiles = range(1, 5) if halo is None else range(6)
    inside = (lane & 4) == 0
    for p in planes[0]:
        for f in range(5):
            own = None
            if halo is not None:
                near = halo[(f * 4 + p) * 8 : (f * 4 + p) * 8 + 8, :]
                s[p, f, 4:8, :] = near[4:]
                s[p, f, 40:44, :] = near[:4]
                own = roll(near, 4, 1)
            for tile in range(1, 5):
                v = source(blocks, f, p, 8 * tile - 8, 8)
                s[p, f, 8 * tile : 8 * tile + 8, :] = v
                v = roll(v, tile * 8 + 4, 1)
                own = v if own is None else jnp.where(lane >= tile * 8, v, own)
            v, base = zcolumns(blocks, zrecv, f, p)
            other = roll(v, 8 - base, 1)
            if halo is not None:
                own = jnp.where(lane >= 40, roll(near, 44, 1), own)
                edge = halo[160 + 8 * f : 168 + 8 * f, :]
                other = jnp.where(lane < 8, roll(edge, -p * 8, 1), other)
                other = jnp.where(lane >= 40, roll(edge, 40 - p * 8, 1), other)
            hs[p, f] = jnp.where(inside, other, own)
            xs[p, f] = jnp.where(inside, own, other)
    for p in planes[0]:
        for f in range(5):
            hs[p, f] = jnp.where(lane < 64, hs[p, f], roll(xs[p, f], 64, 1))
    for p in planes[0]:
        for q, v in enumerate(equilibrium(hs[p, 0], [hs[p, i] for i in (1, 2, 3)])):
            columns_of[0][p, q] = v
        for t in range(4):
            at = slice(8 + 8 * t, 16 + 8 * t)
            for q, v in enumerate(equilibrium(s[p, 0, at, :], [s[p, i, at, :] for i in (1, 2, 3)])):
                levels[0][p, q, at, :] = v
        if halo is not None:
            start_frame(s, levels[0], p)
    for step in range(3):
        src, dst = levels[step], levels[step + 1]
        advance_columns(columns_of[step], columns_of[step + 1], hs, xs, inj, planes[step + 1], tiles)
        for p in planes[step + 1]:
            for t in range(4):
                at = slice(8 + 8 * t, 16 + 8 * t)
                for q, v in enumerate(collide(main_pull(src, inj, p, t), s[p, 4, at, :])):
                    dst[p, q, at, :] = v
            if halo is not None:
                advance_frame(src, dst, s, inj, p, 4)


def start_frame(s, g, p):
    parts = [framed(s, (p, i), 4) for i in range(4)]
    for q, v in enumerate(equilibrium(parts[0], parts[1:])):
        put_framed(g, (p, q), 4, v)


def advance_frame(src, dst, s, inj, p, radius):
    for q, v in enumerate(collide(frame_pull(src, inj, p, radius), framed(s, (p, 4), radius))):
        put_framed(dst, (p, q), radius, v)


NEAR = [range(4, 12), range(5, 11), range(6, 10), range(7, 9)]
FAR = [range(0, 4), range(1, 5), range(2, 6), range(3, 7)]


def near_kernel(first_own, rest_own, zrecv, first_pair, rest_pair, s, hs, g0, g1, g2, g3, ha, hb, xs, inj):
    blocks = ((first_own, rest_own), (first_pair, rest_pair), None)
    inner(blocks, zrecv, NEAR, s, hs, (g0, g1, g2, g3), (ha, hb, ha, hb), xs, inj)


def frame_kernel(from_core, from_chip, *refs):
    s, hs, g0, g1, g2, g3, h0, h1, h2, h3, ls, xs, inj = refs[6:]
    lane = lanes()
    inside = (lane & 4) == 0
    slot = lane & 56
    added = (slot == 0) | (slot == 40)
    for f in range(5):
        edge = y_halo(from_core, from_chip, 160 + f * 4)
        for p in NEAR[0]:
            v = y_halo(from_core, from_chip, (f * 8 + p - 4) * 4)
            s[p, f, 4:8, :] = v[4:]
            s[p, f, 40:44, :] = v[:4]
            own = jnp.where(lane < 8, roll(v, 4, 1), roll(v, 44, 1))
            other = jnp.where(lane < 8, roll(edge, -(p - 4) * 8, 1), roll(edge, 40 - (p - 4) * 8, 1))
            ls[p, f] = jnp.where(inside, other, own)
            xs[p, f] = jnp.where(inside, own, other)
    for p in NEAR[0]:
        for f in range(5):
            v = jnp.where(lane < 64, ls[p, f], roll(xs[p, f], 64, 1))
            hs[p, f] = jnp.where(added, v, hs[p, f])
    for p in NEAR[0]:
        for q, v in enumerate(equilibrium(hs[p, 0], [hs[p, i] for i in (1, 2, 3)])):
            h0[p, q] = v
        start_frame(s, g0, p)
    levels, columns_of = [g0, g1, g2, g3], [h0, h1, h2, h3]
    for step in range(3):
        src, dst = levels[step], levels[step + 1]
        advance_columns(columns_of[step], columns_of[step + 1], hs, xs, inj, NEAR[step + 1], (0, 1, 4, 5))
        for p in NEAR[step + 1]:
            advance_frame(src, dst, s, inj, p, 3 - step)


def far_kernel(first_far, rest_far, halo, *refs):
    density, momentum, s, hs, g0, g1, g2, g3, h0, h1, h2, h3, xs, inj = refs[10:]
    blocks = (None, None, (first_far, rest_far))
    inner(blocks, None, FAR, s, hs, (g0, g1, g2, g3), (h0, h1, h2, h3), xs, inj, halo)
    advance_columns(h3, None, hs, xs, inj, range(4, 8), range(1, 5))
    odd = lax.axis_index("gx") % 2
    sign = (1 - 2 * odd).astype(F32)
    for p in range(4):
        plane = p + odd * (3 - 2 * p)
        for t in range(4):
            at = slice(8 * t, 8 * t + 8)
            r, *j = moments(main_pull(g3, inj, p + 4, t))
            density[plane, at, :] = r
            j[0] = j[0] * sign
            for i in range(3):
                momentum[i, plane, at, :] = j[i]


def call(kernel, out_shape, args, *, scratch=(), specs=None, limit=2 * MIB, flops=0, aliases=None):
    cost = pl.CostEstimate(flops=flops, bytes_accessed=0, transcendentals=0) if flops else None
    return pl.pallas_call(
        kernel,
        out_shape=out_shape,
        in_specs=specs or [VMEM] * len(args),
        out_specs=jax.tree.map(lambda _: VMEM, out_shape),
        scratch_shapes=scratch,
        input_output_aliases=aliases or {},
        cost_estimate=cost,
        compiler_params=pltpu.CompilerParams(vmem_limit_bytes=limit),
    )(*args)


def local(density, velocity, solid_mask):
    hbm = pl.BlockSpec(memory_space=pltpu.HBM)
    block, rest, zcols = call(
        pack_kernel,
        (pltpu.VMEM((3, 4, 32, 128), F32), pltpu.VMEM((2, 4, 32, 128), F32), pltpu.VMEM((40, 128), F32)),
        (density, velocity, solid_mask),
        specs=[hbm] * 3,
        scratch=[
            pltpu.VMEM((4, 32, 128), F32),
            pltpu.VMEM((3, 4, 32, 128), F32),
            pltpu.VMEM((4, 32, 128), jnp.int32),
            pltpu.SemaphoreType.DMA((3,)),
        ],
        limit=PACK_LIMIT,
    )

    def pair(x, y, z):
        return x ^ 1, y, z

    def relay(x, y, z):
        return (x - 2 if x % 2 else x + 2), y, z

    zrecv = permuted(zcols, lambda x, y, z: (x, y, 1 - z))
    first_pair = permuted(block, pair)
    second = call(second_message_kernel, pltpu.VMEM((296, 128), F32), (rest, zrecv))
    rest_pair = permuted(second, pair)
    first_far = permuted(first_pair, relay)
    rest_far = permuted(rest_pair, relay)
    fields, level = pltpu.VMEM((12, 5, 48, 128), F32), pltpu.VMEM((12, 19, 48, 128), F32)
    column_fields, column_level = pltpu.VMEM((12, 5, 8, 128), F32), pltpu.VMEM((12, 19, 8, 128), F32)
    injected = pltpu.VMEM((12, 5, 48, 128), F32)
    state = (fields, column_fields) + (level,) * 4
    to_core, to_chip = call(
        y_message_kernel, (pltpu.VMEM((184, 128), F32),) * 2, (block, rest, zrecv, first_pair, rest_pair)
    )
    from_core = permuted(to_core, lambda x, y, z: (x, y ^ 1, z))
    from_chip = permuted(to_chip, lambda x, y, z: (x, y + 1 if y % 2 else y - 1, z))
    near = call(
        near_kernel,
        state,
        (block, rest, zrecv, first_pair, rest_pair),
        scratch=[column_level, column_level, column_fields, injected],
        limit=6 * MIB,
        flops=INNER_FLOPS,
    )
    halo_far = permuted(call(halo_message_kernel, pltpu.VMEM((200, 128), F32), (from_core, from_chip, near[1])), relay)
    near = call(
        frame_kernel,
        state + (column_level,) * 4,
        (from_core, from_chip, *near),
        scratch=[column_fields, column_fields, injected],
        limit=4 * MIB,
        flops=INNER_FLOPS,
        aliases={2 + i: i for i in range(6)},
    )
    outs = (jax.ShapeDtypeStruct((4, 32, 128), F32), jax.ShapeDtypeStruct((3, 4, 32, 128), F32))
    return tuple(
        call(
            far_kernel,
            outs + state + (column_level,) * 4,
            (first_far, rest_far, halo_far, *near),
            scratch=[column_fields, injected],
            limit=4 * MIB,
            flops=INNER_FLOPS,
            aliases={3 + i: 2 + i for i in range(10)},
        )[:2]
    )


def solution(mesh):
    placed = (P("gx", "gy", "gz"), P(None, "gx", "gy", "gz"), P("gx", "gy", "gz"))
    return jax.shard_map(
        local,
        mesh=mesh,
        in_specs=placed,
        out_specs=(P("gx", "gy", "gz"), P(None, "gx", "gy", "gz")),
        check_vma=False,
    )
```

profile of v0, /device:TPU:0, one launch (start us, length us, event | category | flops | bytes accessed | tf_op | source)
XLA Modules:
  0.0 38.0 jit_solution(11990401365977385251)
XLA Ops:
  0.6 1.2 %shard_map.50 = (f32[3,4,32,128]{3,2,1,0:T(8,128)S(1)}, f32[2,4,32,128]{3,2,1,0:T(8,128)S(1)}, f32[40,128]{1,0:T(8,128)S(1)}) custom-call(f32[4,32,128]{2,1,0:T(8,128)} %d_hbm.1, f32[3,4,32,128]{3,2,1,0:T(8,128)} %v_hbm.1, s32[4,32,128]{2,1,0:T(8,128)} %m_hbm.1), custom_call_target="tpu_custom_call" | custom-call | tf_op jit(solution)/shard_map/pallas_call | solution.py:426
  1.8 4.1 %collective-permute-start = (f32[3,4,32,128]{3,2,1,0:T(8,128)S(1)}, f32[3,4,32,128]{3,2,1,0:T(8,128)S(1)}, u32[]{:S(2)}, u32[]{:S(2)}) collective-permute-start(f32[3,4,32,128]{3,2,1,0:T(8,128)S(1)} %get-tuple-element.25.first_own), channel_id=1, source_target_pairs={{0,16},{1,17},{2,18},{3,19},{4,20},{5,21},{6,22},{7,23},{8,24},{9,... | collective-permute-start | bytes 589832 | tf_op jit(solution)/shard_map/ppermute | solution.py:60
  5.9 1.0 %collective-permute-start.2 = (f32[40,128]{1,0:T(8,128)S(1)}, f32[40,128]{1,0:T(8,128)S(1)}, u32[]{:S(2)}, u32[]{:S(2)}) collective-permute-start(f32[40,128]{1,0:T(8,128)S(1)} %get-tuple-element.27), channel_id=1, source_target_pairs={{0,1},{1,0},{2,3},{3,2},{4,5},{5,4},{6,7},{7,6},{8,9},{9,8},{10,11... | collective-permute-start | bytes 61448 | tf_op jit(solution)/shard_map/ppermute | solution.py:60
  6.9 5.1 %collective-permute-done.2.zrecv = f32[40,128]{1,0:T(8,128)S(1)} collective-permute-done((f32[40,128]{1,0:T(8,128)S(1)}, f32[40,128]{1,0:T(8,128)S(1)}, u32[]{:S(2)}, u32[]{:S(2)}) %collective-permute-start.2) | collective-permute-done | bytes 20512 | tf_op jit(solution)/shard_map/ppermute | solution.py:60
  11.9 1.2 %collective-permute-start.3 = (f32[296,128]{1,0:T(8,128)S(1)}, f32[296,128]{1,0:T(8,128)S(1)}, u32[]{:S(2)}, u32[]{:S(2)}) collective-permute-start(f32[296,128]{1,0:T(8,128)S(1)} %shard_map.51), channel_id=1, source_target_pairs={{0,16},{1,17},{2,18},{3,19},{4,20},{5,21},{6,22},{7,23},{8,24},{9,... | collective-permute-start | bytes 454664 | tf_op jit(solution)/shard_map/ppermute | solution.py:60
  13.2 5.5 %collective-permute-done.3.rest_pair = f32[296,128]{1,0:T(8,128)S(1)} collective-permute-done((f32[296,128]{1,0:T(8,128)S(1)}, f32[296,128]{1,0:T(8,128)S(1)}, u32[]{:S(2)}, u32[]{:S(2)}) %collective-permute-start.3) | collective-permute-done | bytes 151584 | tf_op jit(solution)/shard_map/ppermute | solution.py:60
  18.7 0.0 collective-permute-done.first_pair
  18.7 0.1 shard_map.52
  18.9 0.1 collective-permute-start.5
  19.0 2.9 %collective-permute-start.6 = (f32[184,128]{1,0:T(8,128)S(1)}, f32[184,128]{1,0:T(8,128)S(1)}, u32[]{:S(2)}, u32[]{:S(2)}) collective-permute-start(f32[184,128]{1,0:T(8,128)S(1)} %get-tuple-element.29), channel_id=1, source_target_pairs={{0,14},{1,15},{2,4},{3,5},{4,2},{5,3},{6,8},{7,9},{8,6},{9,7},{10,... | collective-permute-start | bytes 282632 | tf_op jit(solution)/shard_map/ppermute | solution.py:60
  21.8 1.6 %collective-permute-start.1 = (f32[3,4,32,128]{3,2,1,0:T(8,128)S(1)}, f32[3,4,32,128]{3,2,1,0:T(8,128)S(1)}, u32[]{:S(2)}, u32[]{:S(2)}) collective-permute-start(f32[3,4,32,128]{3,2,1,0:T(8,128)S(1)} %collective-permute-done.first_pair), channel_id=1, source_target_pairs={{0,32},{1,33},{2,34},{3,35},{4,36},{5,37},{6,38},{7,39},{8,40},{9,... | collective-permute-start | bytes 589832 | tf_op jit(solution)/shard_map/ppermute | solution.py:60
  23.4 1.6 %collective-permute-start.4 = (f32[296,128]{1,0:T(8,128)S(1)}, f32[296,128]{1,0:T(8,128)S(1)}, u32[]{:S(2)}, u32[]{:S(2)}) collective-permute-start(f32[296,128]{1,0:T(8,128)S(1)} %collective-permute-done.3.rest_pair), channel_id=1, source_target_pairs={{0,32},{1,33},{2,34},{3,35},{4,36},{5,37},{6,38},{7,39},{8,40},{9,... | collective-permute-start | bytes 454664 | tf_op jit(solution)/shard_map/ppermute | solution.py:60
  25.0 2.5 %shard_map.53 = (f32[12,5,48,128]{3,2,1,0:T(8,128)S(1)}, f32[12,5,8,128]{3,2,1,0:T(8,128)S(1)}, f32[12,19,48,128]{3,2,1,0:T(8,128)S(1)}, f32[12,19,48,128]{3,2,1...) custom-call(f32[3,4,32,128]{3,2,1,0:T(8,128)S(1)} %get-tuple-element.25.first_own, ...), custom_call_target="tpu_custom_call" | custom-call | flops 100000000 | tf_op jit(solution)/shard_map/pallas_call | solution.py:426
  27.5 0.0 collective-permute-done.5.from_core
  27.5 0.0 collective-permute-done.6.from_chip
  27.5 0.1 shard_map.54
  27.6 1.3 %collective-permute-start.7 = (f32[200,128]{1,0:T(8,128)S(1)}, f32[200,128]{1,0:T(8,128)S(1)}, u32[]{:S(2)}, u32[]{:S(2)}) collective-permute-start(f32[200,128]{1,0:T(8,128)S(1)} %shard_map.54), channel_id=1, source_target_pairs={{0,32},{1,33},{2,34},{3,35},{4,36},{5,37},{6,38},{7,39},{8,40},{9,... | collective-permute-start | bytes 307208 | tf_op jit(solution)/shard_map/ppermute | solution.py:60
  28.9 1.4 %shard_map.55 = (f32[12,5,48,128]{3,2,1,0:T(8,128)S(1)}, f32[12,5,8,128]{3,2,1,0:T(8,128)S(1)}, f32[12,19,48,128]{3,2,1,0:T(8,128)S(1)}, f32[12,19,48,128]{3,2,1...) custom-call(f32[184,128]{1,0:T(8,128)S(1)} %collective-permute-done., ...), custom_call_target="tpu_custom_call", output_to_operand_aliasing={{0}: (2, {}), {1}: (3, {}), {2}: (4, {}), {3}: (5, {}), {4}... | custom-call | flops 100000000 | tf_op jit(solution)/shard_map/pallas_call | solution.py:426
  30.3 2.8 %collective-permute-done.4.rest_far = f32[296,128]{1,0:T(8,128)S(1)} collective-permute-done((f32[296,128]{1,0:T(8,128)S(1)}, f32[296,128]{1,0:T(8,128)S(1)}, u32[]{:S(2)}, u32[]{:S(2)}) %collective-permute-start.4) | collective-permute-done | bytes 151584 | tf_op jit(solution)/shard_map/ppermute | solution.py:60
  33.1 0.0 collective-permute-done.1.first_far
  33.1 1.1 %collective-permute-done.7.halo = f32[200,128]{1,0:T(8,128)S(1)} collective-permute-done((f32[200,128]{1,0:T(8,128)S(1)}, f32[200,128]{1,0:T(8,128)S(1)}, u32[]{:S(2)}, u32[]{:S(2)}) %collective-permute-start.7) | collective-permute-done | bytes 102432 | tf_op jit(solution)/shard_map/ppermute | solution.py:60
  34.2 3.8 %shard_map.56 = (f32[4,32,128]{2,1,0:T(8,128)}, f32[3,4,32,128]{3,2,1,0:T(8,128)}, f32[12,5,48,128]{3,2,1,0:T(8,128)S(1)}, f32[12,5,8,128]{3,2,1,0:T(8,128)S(1)}...) custom-call(f32[3,4,32,128]{3,2,1,0:T(8,128)S(1)} %collective-permut, ...), custom_call_target="tpu_custom_call", output_to_operand_aliasing={{2}: (3, {}), {3}: (4, {}), {4}: (5, {}), {5}: (6, {}), {6}... | custom-call | flops 100000000 | tf_op jit(solution)/shard_map/pallas_call | solution.py:426
  (1 shorter events, 0.0 us)
Async XLA Ops:
  1.8 16.9 %collective-permute-start = (f32[3,4,32,128]{3,2,1,0:T(8,128)S(1)}, f32[3,4,32,128]{3,2,1,0:T(8,128)S(1)}, u32[]{:S(2)}, u32[]{:S(2)}) collective-permute-start(f32[3,4,32,128]{3,2,1,0:T(8,128)S(1)} %get-tuple-element.25.first_own), channel_id=1, source_target_pairs={{0,16},{1,17},{2,18},{3,19},{4,20},{5,21},{6,22},{7,23},{8,24},{9,... | collective-permute-start | bytes 589832 | tf_op jit(solution)/shard_map/ppermute | solution.py:60
  5.9 6.1 %collective-permute-start.2 = (f32[40,128]{1,0:T(8,128)S(1)}, f32[40,128]{1,0:T(8,128)S(1)}, u32[]{:S(2)}, u32[]{:S(2)}) collective-permute-start(f32[40,128]{1,0:T(8,128)S(1)} %get-tuple-element.27), channel_id=1, source_target_pairs={{0,1},{1,0},{2,3},{3,2},{4,5},{5,4},{6,7},{7,6},{8,9},{9,8},{10,11... | collective-permute-start | bytes 61448 | tf_op jit(solution)/shard_map/ppermute | solution.py:60
  11.9 6.8 %collective-permute-start.3 = (f32[296,128]{1,0:T(8,128)S(1)}, f32[296,128]{1,0:T(8,128)S(1)}, u32[]{:S(2)}, u32[]{:S(2)}) collective-permute-start(f32[296,128]{1,0:T(8,128)S(1)} %shard_map.51), channel_id=1, source_target_pairs={{0,16},{1,17},{2,18},{3,19},{4,20},{5,21},{6,22},{7,23},{8,24},{9,... | collective-permute-start | bytes 454664 | tf_op jit(solution)/shard_map/ppermute | solution.py:60
  18.9 8.6 %collective-permute-start.5 = (f32[184,128]{1,0:T(8,128)S(1)}, f32[184,128]{1,0:T(8,128)S(1)}, u32[]{:S(2)}, u32[]{:S(2)}) collective-permute-start(f32[184,128]{1,0:T(8,128)S(1)} %get-tuple-element.28), channel_id=1, source_target_pairs={{0,2},{1,3},{2,0},{3,1},{4,6},{5,7},{6,4},{7,5},{8,10},{9,11},{10,... | collective-permute-start | bytes 282632 | tf_op jit(solution)/shard_map/ppermute | solution.py:60
  19.0 8.5 %collective-permute-start.6 = (f32[184,128]{1,0:T(8,128)S(1)}, f32[184,128]{1,0:T(8,128)S(1)}, u32[]{:S(2)}, u32[]{:S(2)}) collective-permute-start(f32[184,128]{1,0:T(8,128)S(1)} %get-tuple-element.29), channel_id=1, source_target_pairs={{0,14},{1,15},{2,4},{3,5},{4,2},{5,3},{6,8},{7,9},{8,6},{9,7},{10,... | collective-permute-start | bytes 282632 | tf_op jit(solution)/shard_map/ppermute | solution.py:60
  21.8 11.3 %collective-permute-start.1 = (f32[3,4,32,128]{3,2,1,0:T(8,128)S(1)}, f32[3,4,32,128]{3,2,1,0:T(8,128)S(1)}, u32[]{:S(2)}, u32[]{:S(2)}) collective-permute-start(f32[3,4,32,128]{3,2,1,0:T(8,128)S(1)} %collective-permute-done.first_pair), channel_id=1, source_target_pairs={{0,32},{1,33},{2,34},{3,35},{4,36},{5,37},{6,38},{7,39},{8,40},{9,... | collective-permute-start | bytes 589832 | tf_op jit(solution)/shard_map/ppermute | solution.py:60
  23.4 9.7 %collective-permute-start.4 = (f32[296,128]{1,0:T(8,128)S(1)}, f32[296,128]{1,0:T(8,128)S(1)}, u32[]{:S(2)}, u32[]{:S(2)}) collective-permute-start(f32[296,128]{1,0:T(8,128)S(1)} %collective-permute-done.3.rest_pair), channel_id=1, source_target_pairs={{0,32},{1,33},{2,34},{3,35},{4,36},{5,37},{6,38},{7,39},{8,40},{9,... | collective-permute-start | bytes 454664 | tf_op jit(solution)/shard_map/ppermute | solution.py:60
  27.6 6.6 %collective-permute-start.7 = (f32[200,128]{1,0:T(8,128)S(1)}, f32[200,128]{1,0:T(8,128)S(1)}, u32[]{:S(2)}, u32[]{:S(2)}) collective-permute-start(f32[200,128]{1,0:T(8,128)S(1)} %shard_map.54), channel_id=1, source_target_pairs={{0,32},{1,33},{2,34},{3,35},{4,36},{5,37},{6,38},{7,39},{8,40},{9,... | collective-permute-start | bytes 307208 | tf_op jit(solution)/shard_map/ppermute | solution.py:60
where the time goes:
time: 38.1 us; the launch traced here: 38 us
  waiting for transfers between devices  14.4 us (38%)
  starting transfers between devices  13.7 us (36%)
  Pallas kernels  9.14 us (24%)
  between operations  0.7 us (2%)
    ppermute x8, waiting for transfers between devices, permuted(): return lax.ppermute(x, AXES, pairs)  14.4 us
    ppermute x8, starting transfers between devices, permuted(): return lax.ppermute(x, AXES, pairs)  13.7 us
    pallas_call x7, Pallas kernels, call(): pl.pallas_call(kernel, out_shape=out_shape, in_specs=specs or [VMEM] * le...  9.14 us
  transfers between devices with their start and end apart: 8, of which 4 were waited for; matrix products, arithmetic and copies ran while one was open for 0% of the time, Pallas kernels for 11%

commit v1 on v0

--- a/solution.py
+++ b/solution.py
@@ -122,7 +122,7 @@
     return (-v if f == 1 else v), ((11 - p) if p >= 8 else (3 - p)) * 32
 
 
-def y_message_kernel(first_own, rest_own, zrecv, first_pair, rest_pair, to_core, to_chip):
+def y_message_kernel(first_own, rest_own, zrecv, first_pair, rest_pair, _, to_core, to_chip):
     blocks = ((first_own, rest_own), (first_pair, rest_pair), None)
     first = lax.axis_index("gy") % 2 == 0
     lane = lanes()
@@ -301,30 +301,20 @@
     return [r] + momentum_of([f[a] - f[b] for a, b in PAIRS])
 
 
-def inner(blocks, zrecv, planes, s, hs, levels, columns_of, xs, inj, halo=None):
+def inner(blocks, zrecv, planes, s, hs, levels, columns_of, xs, inj):
     lane = lanes()
-    tiles = range(1, 5) if halo is None else range(6)
+    tiles = range(1, 5)
     inside = (lane & 4) == 0
     for p in planes[0]:
         for f in range(5):
             own = None
-            if halo is not None:
-                near = halo[(f * 4 + p) * 8 : (f * 4 + p) * 8 + 8, :]
-                s[p, f, 4:8, :] = near[4:]
-                s[p, f, 40:44, :] = near[:4]
-                own = roll(near, 4, 1)
-            for tile in range(1, 5):
+            for tile in tiles:
                 v = source(blocks, f, p, 8 * tile - 8, 8)
                 s[p, f, 8 * tile : 8 * tile + 8, :] = v
                 v = roll(v, tile * 8 + 4, 1)
                 own = v if own is None else jnp.where(lane >= tile * 8, v, own)
             v, base = zcolumns(blocks, zrecv, f, p)
             other = roll(v, 8 - base, 1)
-            if halo is not None:
-                own = jnp.where(lane >= 40, roll(near, 44, 1), own)
-                edge = halo[160 + 8 * f : 168 + 8 * f, :]
-                other = jnp.where(lane < 8, roll(edge, -p * 8, 1), other)
-                other = jnp.where(lane >= 40, roll(edge, 40 - p * 8, 1), other)
             hs[p, f] = jnp.where(inside, other, own)
             xs[p, f] = jnp.where(inside, own, other)
     for p in planes[0]:
@@ -337,8 +327,6 @@
             at = slice(8 + 8 * t, 16 + 8 * t)
             for q, v in enumerate(equilibrium(s[p, 0, at, :], [s[p, i, at, :] for i in (1, 2, 3)])):
                 levels[0][p, q, at, :] = v
-        if halo is not None:
-            start_frame(s, levels[0], p)
     for step in range(3):
         src, dst = levels[step], levels[step + 1]
         advance_columns(columns_of[step], columns_of[step + 1], hs, xs, inj, planes[step + 1], tiles)
@@ -347,8 +335,6 @@
                 at = slice(8 + 8 * t, 16 + 8 * t)
                 for q, v in enumerate(collide(main_pull(src, inj, p, t), s[p, 4, at, :])):
                     dst[p, q, at, :] = v
-            if halo is not None:
-                advance_frame(src, dst, s, inj, p, 4)
 
 
 def start_frame(s, g, p):
@@ -362,63 +348,90 @@
         put_framed(dst, (p, q), radius, v)
 
 
+OWN = [range(4, 8), range(5, 7), (), ()]
+PAIR = [range(8, 12), range(7, 11), range(6, 10), range(7, 9)]
 NEAR = [range(4, 12), range(5, 11), range(6, 10), range(7, 9)]
 FAR = [range(0, 4), range(1, 5), range(2, 6), range(3, 7)]
 
 
-def near_kernel(first_own, rest_own, zrecv, first_pair, rest_pair, s, hs, g0, g1, g2, g3, ha, hb, xs, inj):
-    blocks = ((first_own, rest_own), (first_pair, rest_pair), None)
-    inner(blocks, zrecv, NEAR, s, hs, (g0, g1, g2, g3), (ha, hb, ha, hb), xs, inj)
-
-
-def frame_kernel(from_core, from_chip, *refs):
-    s, hs, g0, g1, g2, g3, h0, h1, h2, h3, ls, xs, inj = refs[6:]
+def own_kernel(first_own, rest_own, zrecv, s, hs, g0, g1, g2, g3, h0, h1, h2, h3, xs, inj):
+    inner(((first_own, rest_own), None, None), zrecv, OWN, s, hs, (g0, g1, g2, g3), (h0, h1, h2, h3), xs, inj)
+
+
+def pair_kernel(first_pair, rest_pair, *refs):
+    s, hs, g0, g1, g2, g3, h0, h1, h2, h3, xs, inj = refs[10:]
+    inner((None, (first_pair, rest_pair), None), None, PAIR, s, hs, (g0, g1, g2, g3), (h0, h1, h2, h3), xs, inj)
+
+
+def far_kernel(first_far, rest_far, *refs):
+    s, hs, g0, g1, g2, g3, h0, h1, h2, h3, mid, xs, inj = refs[10:]
+    inner((None, None, (first_far, rest_far)), None, FAR, s, hs, (g0, g1, g2, g3), (h0, h1, h2, h3), xs, inj)
+    advance_columns(h3, None, hs, xs, inj, range(4, 8), range(1, 5))
+    for p in range(4):
+        for t in range(4):
+            for i, v in enumerate(moments(main_pull(g3, inj, p + 4, t))):
+                mid[i, p, 8 * t : 8 * t + 8, :] = v
+
+
+def frames(halo, edge, planes, s, hs, levels, columns_of, ls, xs, inj):
     lane = lanes()
     inside = (lane & 4) == 0
     slot = lane & 56
     added = (slot == 0) | (slot == 40)
     for f in range(5):
-        edge = y_halo(from_core, from_chip, 160 + f * 4)
-        for p in NEAR[0]:
-            v = y_halo(from_core, from_chip, (f * 8 + p - 4) * 4)
+        packed = edge(f)
+        for p in planes[0]:
+            v = halo(f, p)
             s[p, f, 4:8, :] = v[4:]
             s[p, f, 40:44, :] = v[:4]
             own = jnp.where(lane < 8, roll(v, 4, 1), roll(v, 44, 1))
-            other = jnp.where(lane < 8, roll(edge, -(p - 4) * 8, 1), roll(edge, 40 - (p - 4) * 8, 1))
+            base = (p - planes[0][0]) * 8
+            other = jnp.where(lane < 8, roll(packed, -base, 1), roll(packed, 40 - base, 1))
             ls[p, f] = jnp.where(inside, other, own)
             xs[p, f] = jnp.where(inside, own, other)
-    for p in NEAR[0]:
+    for p in planes[0]:
         for f in range(5):
             v = jnp.where(lane < 64, ls[p, f], roll(xs[p, f], 64, 1))
             hs[p, f] = jnp.where(added, v, hs[p, f])
-    for p in NEAR[0]:
+    for p in planes[0]:
         for q, v in enumerate(equilibrium(hs[p, 0], [hs[p, i] for i in (1, 2, 3)])):
-            h0[p, q] = v
-        start_frame(s, g0, p)
-    levels, columns_of = [g0, g1, g2, g3], [h0, h1, h2, h3]
+            columns_of[0][p, q] = v
+        start_frame(s, levels[0], p)
     for step in range(3):
         src, dst = levels[step], levels[step + 1]
-        advance_columns(columns_of[step], columns_of[step + 1], hs, xs, inj, NEAR[step + 1], (0, 1, 4, 5))
-        for p in NEAR[step + 1]:
+        advance_columns(columns_of[step], columns_of[step + 1], hs, xs, inj, planes[step + 1], (0, 1, 4, 5))
+        for p in planes[step + 1]:
             advance_frame(src, dst, s, inj, p, 3 - step)
 
 
-def far_kernel(first_far, rest_far, halo, *refs):
-    density, momentum, s, hs, g0, g1, g2, g3, h0, h1, h2, h3, xs, inj = refs[10:]
-    blocks = (None, None, (first_far, rest_far))
-    inner(blocks, None, FAR, s, hs, (g0, g1, g2, g3), (h0, h1, h2, h3), xs, inj, halo)
-    advance_columns(h3, None, hs, xs, inj, range(4, 8), range(1, 5))
+def near_frame_kernel(from_core, from_chip, *refs):
+    s, hs, g0, g1, g2, g3, h0, h1, h2, h3, ls, xs, inj = refs[10:]
+    frames(
+        lambda f, p: y_halo(from_core, from_chip, (f * 8 + p - 4) * 4),
+        lambda f: y_halo(from_core, from_chip, 160 + f * 4),
+        NEAR, s, hs, (g0, g1, g2, g3), (h0, h1, h2, h3), ls, xs, inj,
+    )
+
+
+def far_frame_kernel(halo, *refs):
+    mid, density, momentum, s, hs, g0, g1, g2, g3, h0, h1, h2, h3, ls, xs, inj = refs[10:]
+    frames(
+        lambda f, p: halo[(f * 4 + p) * 8 : (f * 4 + p) * 8 + 8, :],
+        lambda f: halo[160 + 8 * f : 168 + 8 * f, :],
+        FAR, s, hs, (g0, g1, g2, g3), (h0, h1, h2, h3), ls, xs, inj,
+    )
+    advance_columns(h3, None, hs, xs, inj, range(4, 8), (1, 4))
     odd = lax.axis_index("gx") % 2
     sign = (1 - 2 * odd).astype(F32)
     for p in range(4):
+        out = moments(frame_pull(g3, inj, p + 4, 0))
         plane = p + odd * (3 - 2 * p)
-        for t in range(4):
-            at = slice(8 * t, 8 * t + 8)
-            r, *j = moments(main_pull(g3, inj, p + 4, t))
-            density[plane, at, :] = r
-            j[0] = j[0] * sign
-            for i in range(3):
-                momentum[i, plane, at, :] = j[i]
+        for i in range(4):
+            ref, index = (density, (plane,)) if i == 0 else (momentum, (i - 1, plane))
+            scale = sign if i == 1 else 1.0
+            ref[index] = mid[i, p] * scale
+            ref[index + (slice(0, 4), slice(None))] = out[i][:4] * scale
+            ref[index + (slice(28, 32), slice(None))] = out[i][4:] * scale
 
 
 def call(kernel, out_shape, args, *, scratch=(), specs=None, limit=2 * MIB, flops=0, aliases=None):
@@ -466,40 +479,41 @@
     fields, level = pltpu.VMEM((12, 5, 48, 128), F32), pltpu.VMEM((12, 19, 48, 128), F32)
     column_fields, column_level = pltpu.VMEM((12, 5, 8, 128), F32), pltpu.VMEM((12, 19, 8, 128), F32)
     injected = pltpu.VMEM((12, 5, 48, 128), F32)
-    state = (fields, column_fields) + (level,) * 4
+    state = (fields, column_fields) + (level,) * 4 + (column_level,) * 4
+    work = [column_fields, injected]
+
+    def stage(kernel, args, state_in, *, extra=(), before=(), scratch=work):
+        count = len(args)
+        return call(
+            kernel,
+            tuple(before) + state + tuple(extra),
+            (*args, *state_in),
+            scratch=scratch,
+            limit=4 * MIB,
+            flops=INNER_FLOPS,
+            aliases={count + i: len(before) + i for i in range(len(state))} if state_in else None,
+        )
+
+    near = stage(own_kernel, (block, rest, zrecv), ())
     to_core, to_chip = call(
-        y_message_kernel, (pltpu.VMEM((184, 128), F32),) * 2, (block, rest, zrecv, first_pair, rest_pair)
+        y_message_kernel, (pltpu.VMEM((184, 128), F32),) * 2, (block, rest, zrecv, first_pair, rest_pair, near[1])
     )
     from_core = permuted(to_core, lambda x, y, z: (x, y ^ 1, z))
     from_chip = permuted(to_chip, lambda x, y, z: (x, y + 1 if y % 2 else y - 1, z))
-    near = call(
-        near_kernel,
-        state,
-        (block, rest, zrecv, first_pair, rest_pair),
-        scratch=[column_level, column_level, column_fields, injected],
-        limit=6 * MIB,
-        flops=INNER_FLOPS,
-    )
+    near = stage(pair_kernel, (first_pair, rest_pair), near)
     halo_far = permuted(call(halo_message_kernel, pltpu.VMEM((200, 128), F32), (from_core, from_chip, near[1])), relay)
-    near = call(
-        frame_kernel,
-        state + (column_level,) * 4,
-        (from_core, from_chip, *near),
-        scratch=[column_fields, column_fields, injected],
-        limit=4 * MIB,
-        flops=INNER_FLOPS,
-        aliases={2 + i: i for i in range(6)},
-    )
+    near = stage(near_frame_kernel, (from_core, from_chip), near, scratch=[column_fields, *work])
+    *far, mid = stage(far_kernel, (first_far, rest_far), near, extra=[pltpu.VMEM((4, 4, 32, 128), F32)])
     outs = (jax.ShapeDtypeStruct((4, 32, 128), F32), jax.ShapeDtypeStruct((3, 4, 32, 128), F32))
     return tuple(
         call(
-            far_kernel,
-            outs + state + (column_level,) * 4,
-            (first_far, rest_far, halo_far, *near),
-            scratch=[column_fields, injected],
+            far_frame_kernel,
+            outs + state,
+            (halo_far, *far, mid),
+            scratch=[column_fields, *work],
             limit=4 * MIB,
             flops=INNER_FLOPS,
-            aliases={3 + i: 2 + i for i in range(10)},
+            aliases={1 + i: 2 + i for i in range(10)},
         )[:2]
     )
 

time: 38.1 us -> 33.5 us (0.88)
  waiting for transfers between devices: 14.4 us -> 8.8 us
  Pallas kernels: 9.14 us -> 9.81 us
    ppermute x8, waiting for transfers between devices: 14.4 us -> 8.8 us  [permuted(): return lax.ppermute(x, AXES, pairs)]
    pallas_call x7 -> x9, Pallas kernels: 9.14 us -> 9.81 us  [call(): pl.pallas_call(kernel, out_shape=out_shape, in_specs=specs or [VMEM] * le...]
  transfers between devices with their start and end apart: 8 -> 8, of which waited for: 4 -> 4; matrix products, arithmetic and copies ran while one was open for 0% -> 0% of each run, Pallas kernels for 11% -> 20%
where the time goes in v1:
time: 33.5 us; the launch traced here: 33.3 us
  starting transfers between devices  14 us (42%)
  Pallas kernels  9.81 us (29%)
  waiting for transfers between devices  8.8 us (26%)
  between operations  0.71 us (2%)
    ppermute x8, starting transfers between devices, permuted(): return lax.ppermute(x, AXES, pairs)  14 us
    pallas_call x9, Pallas kernels, call(): pl.pallas_call(kernel, out_shape=out_shape, in_specs=specs or [VMEM] * le...  9.81 us
    ppermute x8, waiting for transfers between devices, permuted(): return lax.ppermute(x, AXES, pairs)  8.8 us
  transfers between devices with their start and end apart: 8, of which 4 were waited for; matrix products, arithmetic and copies ran while one was open for 0% of the time, Pallas kernels for 20%

profile of v1, /device:TPU:0, one launch (start us, length us, event | category | flops | bytes accessed | tf_op | source)
XLA Modules:
  0.0 33.3 jit_solution(14130347666638296509)
XLA Ops:
  0.6 1.2 %shard_map.50 = (f32[3,4,32,128]{3,2,1,0:T(8,128)S(1)}, f32[2,4,32,128]{3,2,1,0:T(8,128)S(1)}, f32[40,128]{1,0:T(8,128)S(1)}) custom-call(f32[4,32,128]{2,1,0:T(8,128)} %d_hbm.1, f32[3,4,32,128]{3,2,1,0:T(8,128)} %v_hbm.1, s32[4,32,128]{2,1,0:T(8,128)} %m_hbm.1), custom_call_target="tpu_custom_call" | custom-call | tf_op jit(solution)/shard_map/pallas_call | solution.py:439
  1.8 4.1 %collective-permute-start.1 = (f32[3,4,32,128]{3,2,1,0:T(8,128)S(1)}, f32[3,4,32,128]{3,2,1,0:T(8,128)S(1)}, u32[]{:S(2)}, u32[]{:S(2)}) collective-permute-start(f32[3,4,32,128]{3,2,1,0:T(8,128)S(1)} %get-tuple-element.50.first_own), channel_id=1, source_target_pairs={{0,16},{1,17},{2,18},{3,19},{4,20},{5,21},{6,22},{7,23},{8,24},{9,... | collective-permute-start | bytes 589832 | tf_op jit(solution)/shard_map/ppermute | solution.py:60
  5.9 1.0 %collective-permute-start = (f32[40,128]{1,0:T(8,128)S(1)}, f32[40,128]{1,0:T(8,128)S(1)}, u32[]{:S(2)}, u32[]{:S(2)}) collective-permute-start(f32[40,128]{1,0:T(8,128)S(1)} %get-tuple-element.52), channel_id=1, source_target_pairs={{0,1},{1,0},{2,3},{3,2},{4,5},{5,4},{6,7},{7,6},{8,9},{9,8},{10,11... | collective-permute-start | bytes 61448 | tf_op jit(solution)/shard_map/ppermute | solution.py:60
  6.9 5.1 %collective-permute-done.zrecv = f32[40,128]{1,0:T(8,128)S(1)} collective-permute-done((f32[40,128]{1,0:T(8,128)S(1)}, f32[40,128]{1,0:T(8,128)S(1)}, u32[]{:S(2)}, u32[]{:S(2)}) %collective-permute-start) | collective-permute-done | bytes 20512 | tf_op jit(solution)/shard_map/ppermute | solution.py:60
  11.9 1.2 %collective-permute-start.2 = (f32[296,128]{1,0:T(8,128)S(1)}, f32[296,128]{1,0:T(8,128)S(1)}, u32[]{:S(2)}, u32[]{:S(2)}) collective-permute-start(f32[296,128]{1,0:T(8,128)S(1)} %shard_map.51), channel_id=1, source_target_pairs={{0,16},{1,17},{2,18},{3,19},{4,20},{5,21},{6,22},{7,23},{8,24},{9,... | collective-permute-start | bytes 454664 | tf_op jit(solution)/shard_map/ppermute | solution.py:60
  13.2 0.0 collective-permute-done.1.first_pair
  13.2 1.6 %collective-permute-start.6 = (f32[3,4,32,128]{3,2,1,0:T(8,128)S(1)}, f32[3,4,32,128]{3,2,1,0:T(8,128)S(1)}, u32[]{:S(2)}, u32[]{:S(2)}) collective-permute-start(f32[3,4,32,128]{3,2,1,0:T(8,128)S(1)} %collective-permute-done.1.first_pair), channel_id=1, source_target_pairs={{0,32},{1,33},{2,34},{3,35},{4,36},{5,37},{6,38},{7,39},{8,40},{9,... | collective-permute-start | bytes 589832 | tf_op jit(solution)/shard_map/ppermute | solution.py:60
  14.8 0.7 %shard_map.52 = (f32[12,5,48,128]{3,2,1,0:T(8,128)S(1)}, f32[12,5,8,128]{3,2,1,0:T(8,128)S(1)}, f32[12,19,48,128]{3,2,1,0:T(8,128)S(1)}, f32[12,19,48,128]{3,2,1...) custom-call(f32[3,4,32,128]{3,2,1,0:T(8,128)S(1)} %get-tuple-element, ...), custom_call_target="tpu_custom_call" | custom-call | flops 100000000 | tf_op jit(solution)/shard_map/pallas_call | solution.py:439
  15.5 3.3 %collective-permute-done.2.rest_pair = f32[296,128]{1,0:T(8,128)S(1)} collective-permute-done((f32[296,128]{1,0:T(8,128)S(1)}, f32[296,128]{1,0:T(8,128)S(1)}, u32[]{:S(2)}, u32[]{:S(2)}) %collective-permute-start.2) | collective-permute-done | bytes 151584 | tf_op jit(solution)/shard_map/ppermute | solution.py:60
  18.7 0.1 shard_map.53
  18.9 0.1 collective-permute-start.3
  18.9 2.9 %collective-permute-start.4 = (f32[184,128]{1,0:T(8,128)S(1)}, f32[184,128]{1,0:T(8,128)S(1)}, u32[]{:S(2)}, u32[]{:S(2)}) collective-permute-start(f32[184,128]{1,0:T(8,128)S(1)} %get-tuple-element.55), channel_id=1, source_target_pairs={{0,14},{1,15},{2,4},{3,5},{4,2},{5,3},{6,8},{7,9},{8,6},{9,7},{10,... | collective-permute-start | bytes 282632 | tf_op jit(solution)/shard_map/ppermute | solution.py:60
  21.8 1.6 %collective-permute-start.7 = (f32[296,128]{1,0:T(8,128)S(1)}, f32[296,128]{1,0:T(8,128)S(1)}, u32[]{:S(2)}, u32[]{:S(2)}) collective-permute-start(f32[296,128]{1,0:T(8,128)S(1)} %collective-permute-done.2.rest_pair), channel_id=1, source_target_pairs={{0,32},{1,33},{2,34},{3,35},{4,36},{5,37},{6,38},{7,39},{8,40},{9,... | collective-permute-start | bytes 454664 | tf_op jit(solution)/shard_map/ppermute | solution.py:60
  23.4 1.9 %shard_map.54 = (f32[12,5,48,128]{3,2,1,0:T(8,128)S(1)}, f32[12,5,8,128]{3,2,1,0:T(8,128)S(1)}, f32[12,19,48,128]{3,2,1,0:T(8,128)S(1)}, f32[12,19,48,128]{3,2,1...) custom-call(f32[3,4,32,128]{3,2,1,0:T(8,128)S(1)} %collective-permut, ...), custom_call_target="tpu_custom_call", output_to_operand_aliasing={{0}: (2, {}), {1}: (3, {}), {2}: (4, {}), {3}: (5, {}), {4}... | custom-call | flops 100000000 | tf_op jit(solution)/shard_map/pallas_call | solution.py:439
  25.3 0.0 collective-permute-done.3.from_core
  25.3 0.0 collective-permute-done.4.from_chip
  25.3 0.1 shard_map.55
  25.4 1.6 %collective-permute-start.5 = (f32[200,128]{1,0:T(8,128)S(1)}, f32[200,128]{1,0:T(8,128)S(1)}, u32[]{:S(2)}, u32[]{:S(2)}) collective-permute-start(f32[200,128]{1,0:T(8,128)S(1)} %shard_map.55), channel_id=1, source_target_pairs={{0,32},{1,33},{2,34},{3,35},{4,36},{5,37},{6,38},{7,39},{8,40},{9,... | collective-permute-start | bytes 307208 | tf_op jit(solution)/shard_map/ppermute | solution.py:60
  27.0 1.4 %shard_map.56 = (f32[12,5,48,128]{3,2,1,0:T(8,128)S(1)}, f32[12,5,8,128]{3,2,1,0:T(8,128)S(1)}, f32[12,19,48,128]{3,2,1,0:T(8,128)S(1)}, f32[12,19,48,128]{3,2,1...) custom-call(f32[184,128]{1,0:T(8,128)S(1)} %collective-permute-done., ...), custom_call_target="tpu_custom_call", output_to_operand_aliasing={{0}: (2, {}), {1}: (3, {}), {2}: (4, {}), {3}: (5, {}), {4}... | custom-call | flops 100000000 | tf_op jit(solution)/shard_map/pallas_call | solution.py:439
  28.3 0.3 collective-permute-done.7.rest_far
  28.7 0.0 collective-permute-done.6.first_far
  28.7 2.4 %shard_map.57 = (f32[12,5,48,128]{3,2,1,0:T(8,128)S(1)}, f32[12,5,8,128]{3,2,1,0:T(8,128)S(1)}, f32[12,19,48,128]{3,2,1,0:T(8,128)S(1)}, f32[12,19,48,128]{3,2,1...) custom-call(f32[3,4,32,128]{3,2,1,0:T(8,128)S(1)} %collective-permut, ...), custom_call_target="tpu_custom_call", output_to_operand_aliasing={{0}: (2, {}), {1}: (3, {}), {2}: (4, {}), {3}: (5, {}), {4}... | custom-call | flops 100000000 | tf_op jit(solution)/shard_map/pallas_call | solution.py:439
  31.1 0.2 collective-permute-done.5.halo
  31.3 2.1 %shard_map.58 = (f32[4,32,128]{2,1,0:T(8,128)}, f32[3,4,32,128]{3,2,1,0:T(8,128)}, f32[12,5,48,128]{3,2,1,0:T(8,128)S(1)}, f32[12,5,8,128]{3,2,1,0:T(8,128)S(1)}...) custom-call(f32[200,128]{1,0:T(8,128)S(1)} %collective-permute-done., ...), custom_call_target="tpu_custom_call", output_to_operand_aliasing={{2}: (1, {}), {3}: (2, {}), {4}: (3, {}), {5}: (4, {}), {6}... | custom-call | flops 100000000 | tf_op jit(solution)/shard_map/pallas_call | solution.py:439
  (1 shorter events, 0.0 us)
Async XLA Ops:
  1.8 11.4 %collective-permute-start.1 = (f32[3,4,32,128]{3,2,1,0:T(8,128)S(1)}, f32[3,4,32,128]{3,2,1,0:T(8,128)S(1)}, u32[]{:S(2)}, u32[]{:S(2)}) collective-permute-start(f32[3,4,32,128]{3,2,1,0:T(8,128)S(1)} %get-tuple-element.50.first_own), channel_id=1, source_target_pairs={{0,16},{1,17},{2,18},{3,19},{4,20},{5,21},{6,22},{7,23},{8,24},{9,... | collective-permute-start | bytes 589832 | tf_op jit(solution)/shard_map/ppermute | solution.py:60
  5.9 6.1 %collective-permute-start = (f32[40,128]{1,0:T(8,128)S(1)}, f32[40,128]{1,0:T(8,128)S(1)}, u32[]{:S(2)}, u32[]{:S(2)}) collective-permute-start(f32[40,128]{1,0:T(8,128)S(1)} %get-tuple-element.52), channel_id=1, source_target_pairs={{0,1},{1,0},{2,3},{3,2},{4,5},{5,4},{6,7},{7,6},{8,9},{9,8},{10,11... | collective-permute-start | bytes 61448 | tf_op jit(solution)/shard_map/ppermute | solution.py:60
  11.9 6.8 %collective-permute-start.2 = (f32[296,128]{1,0:T(8,128)S(1)}, f32[296,128]{1,0:T(8,128)S(1)}, u32[]{:S(2)}, u32[]{:S(2)}) collective-permute-start(f32[296,128]{1,0:T(8,128)S(1)} %shard_map.51), channel_id=1, source_target_pairs={{0,16},{1,17},{2,18},{3,19},{4,20},{5,21},{6,22},{7,23},{8,24},{9,... | collective-permute-start | bytes 454664 | tf_op jit(solution)/shard_map/ppermute | solution.py:60
  13.2 15.5 %collective-permute-start.6 = (f32[3,4,32,128]{3,2,1,0:T(8,128)S(1)}, f32[3,4,32,128]{3,2,1,0:T(8,128)S(1)}, u32[]{:S(2)}, u32[]{:S(2)}) collective-permute-start(f32[3,4,32,128]{3,2,1,0:T(8,128)S(1)} %collective-permute-done.1.first_pair), channel_id=1, source_target_pairs={{0,32},{1,33},{2,34},{3,35},{4,36},{5,37},{6,38},{7,39},{8,40},{9,... | collective-permute-start | bytes 589832 | tf_op jit(solution)/shard_map/ppermute | solution.py:60
  18.9 6.4 %collective-permute-start.3 = (f32[184,128]{1,0:T(8,128)S(1)}, f32[184,128]{1,0:T(8,128)S(1)}, u32[]{:S(2)}, u32[]{:S(2)}) collective-permute-start(f32[184,128]{1,0:T(8,128)S(1)} %get-tuple-element.54), channel_id=1, source_target_pairs={{0,2},{1,3},{2,0},{3,1},{4,6},{5,7},{6,4},{7,5},{8,10},{9,11},{10,... | collective-permute-start | bytes 282632 | tf_op jit(solution)/shard_map/ppermute | solution.py:60
  18.9 6.3 %collective-permute-start.4 = (f32[184,128]{1,0:T(8,128)S(1)}, f32[184,128]{1,0:T(8,128)S(1)}, u32[]{:S(2)}, u32[]{:S(2)}) collective-permute-start(f32[184,128]{1,0:T(8,128)S(1)} %get-tuple-element.55), channel_id=1, source_target_pairs={{0,14},{1,15},{2,4},{3,5},{4,2},{5,3},{6,8},{7,9},{8,6},{9,7},{10,... | collective-permute-start | bytes 282632 | tf_op jit(solution)/shard_map/ppermute | solution.py:60
  21.8 6.9 %collective-permute-start.7 = (f32[296,128]{1,0:T(8,128)S(1)}, f32[296,128]{1,0:T(8,128)S(1)}, u32[]{:S(2)}, u32[]{:S(2)}) collective-permute-start(f32[296,128]{1,0:T(8,128)S(1)} %collective-permute-done.2.rest_pair), channel_id=1, source_target_pairs={{0,32},{1,33},{2,34},{3,35},{4,36},{5,37},{6,38},{7,39},{8,40},{9,... | collective-permute-start | bytes 454664 | tf_op jit(solution)/shard_map/ppermute | solution.py:60
  25.4 5.9 %collective-permute-start.5 = (f32[200,128]{1,0:T(8,128)S(1)}, f32[200,128]{1,0:T(8,128)S(1)}, u32[]{:S(2)}, u32[]{:S(2)}) collective-permute-start(f32[200,128]{1,0:T(8,128)S(1)} %shard_map.55), channel_id=1, source_target_pairs={{0,32},{1,33},{2,34},{3,35},{4,36},{5,37},{6,38},{7,39},{8,40},{9,... | collective-permute-start | bytes 307208 | tf_op jit(solution)/shard_map/ppermute | solution.py:60

commit v2 on v1

--- a/solution.py
+++ b/solution.py
@@ -60,7 +60,7 @@
     return lax.ppermute(x, AXES, pairs)
 
 
-def pack_kernel(d_hbm, v_hbm, m_hbm, block, rest, zcols, d, v, m, sems):
+def pack_kernel(d_hbm, v_hbm, m_hbm, early, late, zcols, d, v, m, sems):
     odd = lax.axis_index("gx") % 2
     sign = (1 - 2 * odd).astype(F32)
     copies = [
@@ -85,45 +85,42 @@
             base = plane * 32 + t * 8
             inside = (lane >= base) & (lane < base + 8)
             for f in range(5):
-                if f < 3:
-                    block[f, plane, at, :] = fields[f]
-                else:
-                    rest[f - 3, plane, at, :] = fields[f]
+                (early if plane > 1 else late)[f, plane % 2, at, :] = fields[f]
                 packed[f] = jnp.where(inside, roll(fields[f], base + 4, 1), packed[f])
     for f in range(5):
         zcols[8 * f : 8 * f + 8, :] = packed[f]
 
 
-def second_message_kernel(rest, zrecv, out):
-    for f in range(2):
-        for plane in range(4):
-            slab = (f * 4 + plane) * 32
-            out[slab : slab + 32, :] = rest[f, plane]
-    out[256:296, :] = zrecv[...]
+def relay_message_kernel(late_pair, zdiag, out):
+    for f in range(5):
+        for plane in range(2):
+            slab = (f * 2 + plane) * 32
+            out[slab : slab + 32, :] = late_pair[f, plane]
+    out[320:360, :] = zdiag[...]
 
 
 def source(blocks, f, p, row, count):
-    first, rest = blocks[(2, 0, 1)[p // 4]]
-    plane = p - 4 if 4 <= p < 8 else (11 - p if p >= 8 else 3 - p)
-    if f < 3:
-        v = first[f, plane, row : row + count, :]
-    elif 4 <= p < 8:
-        v = rest[f - 3, plane, row : row + count, :]
+    early, late, _ = blocks[p // 4]
+    plane = (3 - p, p - 4, 11 - p)[p // 4]
+    if plane > 1:
+        v = early[f, plane - 2, row : row + count, :]
+    elif p >= 4:
+        v = late[f, plane, row : row + count, :]
     else:
-        slab = ((f - 3) * 4 + plane) * 32
-        v = rest[slab + row : slab + row + count, :]
+        slab = (f * 2 + plane) * 32
+        v = late[slab + row : slab + row + count, :]
     return -v if f == 1 and not 4 <= p < 8 else v
 
 
-def zcolumns(blocks, zrecv, f, p):
-    if 4 <= p < 8:
-        return zrecv[8 * f : 8 * f + 8, :], (p - 4) * 32
-    v = blocks[1 if p >= 8 else 2][1][256 + 8 * f : 264 + 8 * f, :]
-    return (-v if f == 1 else v), ((11 - p) if p >= 8 else (3 - p)) * 32
-
-
-def y_message_kernel(first_own, rest_own, zrecv, first_pair, rest_pair, _, to_core, to_chip):
-    blocks = ((first_own, rest_own), (first_pair, rest_pair), None)
+def zcolumns(blocks, f, p):
+    plane = (3 - p, p - 4, 11 - p)[p // 4]
+    start = (320 if p < 4 else 0) + 8 * f
+    v = blocks[p // 4][2][start : start + 8, :]
+    return (-v if f == 1 and not 4 <= p < 8 else v), plane * 32
+
+
+def y_message_kernel(early_own, late_own, zrecv, early_pair, late_pair, zdiag, _, to_core, to_chip):
+    blocks = (None, (early_own, late_own, zrecv), (early_pair, late_pair, zdiag))
     first = lax.axis_index("gy") % 2 == 0
     lane = lanes()
     for f in range(5):
@@ -136,7 +133,7 @@
         edge_low = jnp.zeros((8, 128), F32)
         edge_high = jnp.zeros((8, 128), F32)
         for i in range(8):
-            z, base = zcolumns(blocks, zrecv, f, i + 4)
+            z, base = zcolumns(blocks, f, i + 4)
             inside = (lane >= i * 8) & (lane < i * 8 + 8)
             edge_low = jnp.where(inside, roll(z, i * 8 - base, 1), edge_low)
             edge_high = jnp.where(inside, roll(z, i * 8 - base - 24, 1), edge_high)
@@ -301,7 +298,7 @@
     return [r] + momentum_of([f[a] - f[b] for a, b in PAIRS])
 
 
-def inner(blocks, zrecv, planes, s, hs, levels, columns_of, xs, inj):
+def inner(blocks, planes, s, hs, levels, columns_of, xs, inj):
     lane = lanes()
     tiles = range(1, 5)
     inside = (lane & 4) == 0
@@ -313,7 +310,7 @@
                 s[p, f, 8 * tile : 8 * tile + 8, :] = v
                 v = roll(v, tile * 8 + 4, 1)
                 own = v if own is None else jnp.where(lane >= tile * 8, v, own)
-            v, base = zcolumns(blocks, zrecv, f, p)
+            v, base = zcolumns(blocks, f, p)
             other = roll(v, 8 - base, 1)
             hs[p, f] = jnp.where(inside, other, own)
             xs[p, f] = jnp.where(inside, own, other)
@@ -349,23 +346,29 @@
 
 
 OWN = [range(4, 8), range(5, 7), (), ()]
-PAIR = [range(8, 12), range(7, 11), range(6, 10), range(7, 9)]
+EARLY = [range(8, 10), range(7, 9), range(6, 8), ()]
+LATE = [range(10, 12), range(9, 11), range(8, 10), range(7, 9)]
 NEAR = [range(4, 12), range(5, 11), range(6, 10), range(7, 9)]
 FAR = [range(0, 4), range(1, 5), range(2, 6), range(3, 7)]
 
 
-def own_kernel(first_own, rest_own, zrecv, s, hs, g0, g1, g2, g3, h0, h1, h2, h3, xs, inj):
-    inner(((first_own, rest_own), None, None), zrecv, OWN, s, hs, (g0, g1, g2, g3), (h0, h1, h2, h3), xs, inj)
-
-
-def pair_kernel(first_pair, rest_pair, *refs):
+def own_kernel(early, late, z, s, hs, g0, g1, g2, g3, h0, h1, h2, h3, xs, inj):
+    inner((None, (early, late, z), None), OWN, s, hs, (g0, g1, g2, g3), (h0, h1, h2, h3), xs, inj)
+
+
+def early_kernel(early, z, *refs):
     s, hs, g0, g1, g2, g3, h0, h1, h2, h3, xs, inj = refs[10:]
-    inner((None, (first_pair, rest_pair), None), None, PAIR, s, hs, (g0, g1, g2, g3), (h0, h1, h2, h3), xs, inj)
-
-
-def far_kernel(first_far, rest_far, *refs):
+    inner((None, None, (early, None, z)), EARLY, s, hs, (g0, g1, g2, g3), (h0, h1, h2, h3), xs, inj)
+
+
+def late_kernel(late, z, *refs):
+    s, hs, g0, g1, g2, g3, h0, h1, h2, h3, xs, inj = refs[10:]
+    inner((None, None, (None, late, z)), LATE, s, hs, (g0, g1, g2, g3), (h0, h1, h2, h3), xs, inj)
+
+
+def far_kernel(early, late, *refs):
     s, hs, g0, g1, g2, g3, h0, h1, h2, h3, mid, xs, inj = refs[10:]
-    inner((None, None, (first_far, rest_far)), None, FAR, s, hs, (g0, g1, g2, g3), (h0, h1, h2, h3), xs, inj)
+    inner(((early, late, late), None, None), FAR, s, hs, (g0, g1, g2, g3), (h0, h1, h2, h3), xs, inj)
     advance_columns(h3, None, hs, xs, inj, range(4, 8), range(1, 5))
     for p in range(4):
         for t in range(4):
@@ -450,9 +453,9 @@
 
 def local(density, velocity, solid_mask):
     hbm = pl.BlockSpec(memory_space=pltpu.HBM)
-    block, rest, zcols = call(
+    early, late, zcols = call(
         pack_kernel,
-        (pltpu.VMEM((3, 4, 32, 128), F32), pltpu.VMEM((2, 4, 32, 128), F32), pltpu.VMEM((40, 128), F32)),
+        (pltpu.VMEM((5, 2, 32, 128), F32), pltpu.VMEM((5, 2, 32, 128), F32), pltpu.VMEM((40, 128), F32)),
         (density, velocity, solid_mask),
         specs=[hbm] * 3,
         scratch=[
@@ -470,12 +473,12 @@
     def relay(x, y, z):
         return (x - 2 if x % 2 else x + 2), y, z
 
+    early_pair = permuted(early, pair)
     zrecv = permuted(zcols, lambda x, y, z: (x, y, 1 - z))
-    first_pair = permuted(block, pair)
-    second = call(second_message_kernel, pltpu.VMEM((296, 128), F32), (rest, zrecv))
-    rest_pair = permuted(second, pair)
-    first_far = permuted(first_pair, relay)
-    rest_far = permuted(rest_pair, relay)
+    zdiag = permuted(zcols, lambda x, y, z: (x ^ 1, y, 1 - z))
+    late_pair = permuted(late, pair)
+    early_far = permuted(early_pair, relay)
+    late_far = permuted(call(relay_message_kernel, pltpu.VMEM((360, 128), F32), (late_pair, zdiag)), relay)
     fields, level = pltpu.VMEM((12, 5, 48, 128), F32), pltpu.VMEM((12, 19, 48, 128), F32)
     column_fields, column_level = pltpu.VMEM((12, 5, 8, 128), F32), pltpu.VMEM((12, 19, 8, 128), F32)
     injected = pltpu.VMEM((12, 5, 48, 128), F32)
@@ -494,16 +497,19 @@
             aliases={count + i: len(before) + i for i in range(len(state))} if state_in else None,
         )
 
-    near = stage(own_kernel, (block, rest, zrecv), ())
+    near = stage(own_kernel, (early, late, zrecv), ())
     to_core, to_chip = call(
-        y_message_kernel, (pltpu.VMEM((184, 128), F32),) * 2, (block, rest, zrecv, first_pair, rest_pair, near[1])
+        y_message_kernel,
+        (pltpu.VMEM((184, 128), F32),) * 2,
+        (early, late, zrecv, early_pair, late_pair, zdiag, near[1]),
     )
     from_core = permuted(to_core, lambda x, y, z: (x, y ^ 1, z))
     from_chip = permuted(to_chip, lambda x, y, z: (x, y + 1 if y % 2 else y - 1, z))
-    near = stage(pair_kernel, (first_pair, rest_pair), near)
+    near = stage(early_kernel, (early_pair, zdiag), near)
+    near = stage(late_kernel, (late_pair, zdiag), near)
     halo_far = permuted(call(halo_message_kernel, pltpu.VMEM((200, 128), F32), (from_core, from_chip, near[1])), relay)
     near = stage(near_frame_kernel, (from_core, from_chip), near, scratch=[column_fields, *work])
-    *far, mid = stage(far_kernel, (first_far, rest_far), near, extra=[pltpu.VMEM((4, 4, 32, 128), F32)])
+    *far, mid = stage(far_kernel, (early_far, late_far), near, extra=[pltpu.VMEM((4, 4, 32, 128), F32)])
     outs = (jax.ShapeDtypeStruct((4, 32, 128), F32), jax.ShapeDtypeStruct((3, 4, 32, 128), F32))
     return tuple(
         call(

time: 33.5 us -> 34.6 us (1.033)
  starting transfers between devices: 14 us -> 15.6 us
  waiting for transfers between devices: 8.8 us -> 8.06 us
    ppermute x8 -> x9, starting transfers between devices: 14 us -> 15.6 us  [permuted(): return lax.ppermute(x, AXES, pairs)]
    ppermute x8 -> x9, waiting for transfers between devices: 8.8 us -> 8.06 us  [permuted(): return lax.ppermute(x, AXES, pairs)]
    pallas_call x9 -> x10, Pallas kernels: 9.81 us -> 10 us  [call(): pl.pallas_call(kernel, out_shape=out_shape, in_specs=specs or [VMEM] * le...]
  transfers between devices with their start and end apart: 8 -> 9, of which waited for: 4 -> 2; matrix products, arithmetic and copies ran while one was open for 0% -> 0% of each run, Pallas kernels for 20% -> 19%
where the time goes in v2:
time: 34.6 us; the launch traced here: 34.5 us
  starting transfers between devices  15.6 us (45%)
  Pallas kernels  10 us (29%)
  waiting for transfers between devices  8.06 us (23%)
  between operations  0.75 us (2%)
    ppermute x9, starting transfers between devices, permuted(): return lax.ppermute(x, AXES, pairs)  15.6 us
    pallas_call x10, Pallas kernels, call(): pl.pallas_call(kernel, out_shape=out_shape, in_specs=specs or [VMEM] * le...  10 us
    ppermute x9, waiting for transfers between devices, permuted(): return lax.ppermute(x, AXES, pairs)  8.06 us
  transfers between devices with their start and end apart: 9, of which 2 were waited for; matrix products, arithmetic and copies ran while one was open for 0% of the time, Pallas kernels for 19%

profile of v2, /device:TPU:0, one launch (start us, length us, event | category | flops | bytes accessed | tf_op | source)
XLA Modules:
  0.0 34.5 jit_solution(6225636369055235056)
XLA Ops:
  0.6 1.2 %shard_map.50 = (f32[5,2,32,128]{3,2,1,0:T(8,128)S(1)}, f32[5,2,32,128]{3,2,1,0:T(8,128)S(1)}, f32[40,128]{1,0:T(8,128)S(1)}) custom-call(f32[4,32,128]{2,1,0:T(8,128)} %d_hbm.1, f32[3,4,32,128]{3,2,1,0:T(8,128)} %v_hbm.1, s32[4,32,128]{2,1,0:T(8,128)} %m_hbm.1), custom_call_target="tpu_custom_call" | custom-call | tf_op jit(solution)/shard_map/pallas_call | solution.py:442
  1.8 4.1 %collective-permute-start.1 = (f32[5,2,32,128]{3,2,1,0:T(8,128)S(1)}, f32[5,2,32,128]{3,2,1,0:T(8,128)S(1)}, u32[]{:S(2)}, u32[]{:S(2)}) collective-permute-start(f32[5,2,32,128]{3,2,1,0:T(8,128)S(1)} %get-tuple-element.60.early.early_own), channel_id=1, source_target_pairs={{0,16},{1,17},{2,18},{3,19},{4,20},{5,21},{6,22},{7,23},{8,24},{9,... | collective-permute-start | bytes 491528 | tf_op jit(solution)/shard_map/ppermute | solution.py:60
  5.9 0.1 collective-permute-start.2
  6.0 1.5 %collective-permute-start = (f32[40,128]{1,0:T(8,128)S(1)}, f32[40,128]{1,0:T(8,128)S(1)}, u32[]{:S(2)}, u32[]{:S(2)}) collective-permute-start(f32[40,128]{1,0:T(8,128)S(1)} %get-tuple-element.62), channel_id=1, source_target_pairs={{0,1},{1,0},{2,3},{3,2},{4,5},{5,4},{6,7},{7,6},{8,9},{9,8},{10,11... | collective-permute-start | bytes 61448 | tf_op jit(solution)/shard_map/ppermute | solution.py:60
  7.4 2.5 %collective-permute-start.3 = (f32[40,128]{1,0:T(8,128)S(1)}, f32[40,128]{1,0:T(8,128)S(1)}, u32[]{:S(2)}, u32[]{:S(2)}) collective-permute-start(f32[40,128]{1,0:T(8,128)S(1)} %get-tuple-element.62), channel_id=1, source_target_pairs={{0,17},{1,16},{2,19},{3,18},{4,21},{5,20},{6,23},{7,22},{8,25},{9,... | collective-permute-start | bytes 61448 | tf_op jit(solution)/shard_map/ppermute | solution.py:60
  10.0 4.8 %collective-permute-done.z.zrecv = f32[40,128]{1,0:T(8,128)S(1)} collective-permute-done((f32[40,128]{1,0:T(8,128)S(1)}, f32[40,128]{1,0:T(8,128)S(1)}, u32[]{:S(2)}, u32[]{:S(2)}) %collective-permute-start) | collective-permute-done | bytes 20512 | tf_op jit(solution)/shard_map/ppermute | solution.py:60
  14.8 0.7 %shard_map.51 = (f32[12,5,48,128]{3,2,1,0:T(8,128)S(1)}, f32[12,5,8,128]{3,2,1,0:T(8,128)S(1)}, f32[12,19,48,128]{3,2,1,0:T(8,128)S(1)}, f32[12,19,48,128]{3,2,1...) custom-call(f32[5,2,32,128]{3,2,1,0:T(8,128)S(1)} %get-tuple-element, ...), custom_call_target="tpu_custom_call" | custom-call | flops 100000000 | tf_op jit(solution)/shard_map/pallas_call | solution.py:442
  15.5 0.0 collective-permute-done.3.zdiag.z
  15.5 0.0 collective-permute-done.1.early_pair.early
  15.5 0.0 collective-permute-done.2.late_pair.late
  15.5 0.1 shard_map.52
  15.7 0.1 collective-permute-start.4
  15.7 2.9 %collective-permute-start.5 = (f32[184,128]{1,0:T(8,128)S(1)}, f32[184,128]{1,0:T(8,128)S(1)}, u32[]{:S(2)}, u32[]{:S(2)}) collective-permute-start(f32[184,128]{1,0:T(8,128)S(1)} %get-tuple-element.65), channel_id=1, source_target_pairs={{0,14},{1,15},{2,4},{3,5},{4,2},{5,3},{6,8},{7,9},{8,6},{9,7},{10,... | collective-permute-start | bytes 282632 | tf_op jit(solution)/shard_map/ppermute | solution.py:60
  18.6 1.6 %collective-permute-start.8 = (f32[360,128]{1,0:T(8,128)S(1)}, f32[360,128]{1,0:T(8,128)S(1)}, u32[]{:S(2)}, u32[]{:S(2)}) collective-permute-start(f32[360,128]{1,0:T(8,128)S(1)} %shard_map.56), channel_id=1, source_target_pairs={{0,32},{1,33},{2,34},{3,35},{4,36},{5,37},{6,38},{7,39},{8,40},{9,... | collective-permute-start | bytes 552968 | tf_op jit(solution)/shard_map/ppermute | solution.py:60
  20.3 1.6 %collective-permute-start.7 = (f32[5,2,32,128]{3,2,1,0:T(8,128)S(1)}, f32[5,2,32,128]{3,2,1,0:T(8,128)S(1)}, u32[]{:S(2)}, u32[]{:S(2)}) collective-permute-start(f32[5,2,32,128]{3,2,1,0:T(8,128)S(1)} %collective-permute-done.1.early_pair.early), channel_id=1, source_target_pairs={{0,32},{1,33},{2,34},{3,35},{4,36},{5,37},{6,38},{7,39},{8,40},{9,... | collective-permute-start | bytes 491528 | tf_op jit(solution)/shard_map/ppermute | solution.py:60
  21.8 0.9 %shard_map.53 = (f32[12,5,48,128]{3,2,1,0:T(8,128)S(1)}, f32[12,5,8,128]{3,2,1,0:T(8,128)S(1)}, f32[12,19,48,128]{3,2,1,0:T(8,128)S(1)}, f32[12,19,48,128]{3,2,1...) custom-call(f32[5,2,32,128]{3,2,1,0:T(8,128)S(1)} %collective-permut, ...), custom_call_target="tpu_custom_call", output_to_operand_aliasing={{0}: (2, {}), {1}: (3, {}), {2}: (4, {}), {3}: (5, {}), {4}... | custom-call | flops 100000000 | tf_op jit(solution)/shard_map/pallas_call | solution.py:442
  22.7 1.2 %shard_map.54 = (f32[12,5,48,128]{3,2,1,0:T(8,128)S(1)}, f32[12,5,8,128]{3,2,1,0:T(8,128)S(1)}, f32[12,19,48,128]{3,2,1,0:T(8,128)S(1)}, f32[12,19,48,128]{3,2,1...) custom-call(f32[5,2,32,128]{3,2,1,0:T(8,128)S(1)} %collective-permut, ...), custom_call_target="tpu_custom_call", output_to_operand_aliasing={{0}: (2, {}), {1}: (3, {}), {2}: (4, {}), {3}: (5, {}), {4}... | custom-call | flops 100000000 | tf_op jit(solution)/shard_map/pallas_call | solution.py:442
  23.9 0.0 collective-permute-done.4.from_core
  23.9 0.0 collective-permute-done.5.from_chip
  24.0 0.1 shard_map.55
  24.1 1.3 %collective-permute-start.6 = (f32[200,128]{1,0:T(8,128)S(1)}, f32[200,128]{1,0:T(8,128)S(1)}, u32[]{:S(2)}, u32[]{:S(2)}) collective-permute-start(f32[200,128]{1,0:T(8,128)S(1)} %shard_map.55), channel_id=1, source_target_pairs={{0,32},{1,33},{2,34},{3,35},{4,36},{5,37},{6,38},{7,39},{8,40},{9,... | collective-permute-start | bytes 307208 | tf_op jit(solution)/shard_map/ppermute | solution.py:60
  25.4 1.4 %shard_map.57 = (f32[12,5,48,128]{3,2,1,0:T(8,128)S(1)}, f32[12,5,8,128]{3,2,1,0:T(8,128)S(1)}, f32[12,19,48,128]{3,2,1,0:T(8,128)S(1)}, f32[12,19,48,128]{3,2,1...) custom-call(f32[184,128]{1,0:T(8,128)S(1)} %collective-permute-done., ...), custom_call_target="tpu_custom_call", output_to_operand_aliasing={{0}: (2, {}), {1}: (3, {}), {2}: (4, {}), {3}: (5, {}), {4}... | custom-call | flops 100000000 | tf_op jit(solution)/shard_map/pallas_call | solution.py:442
  26.7 3.2 %collective-permute-done.7.early = f32[5,2,32,128]{3,2,1,0:T(8,128)S(1)} collective-permute-done((f32[5,2,32,128]{3,2,1,0:T(8,128)S(1)}, f32[5,2,32,128]{3,2,1,0:T(8,128)S(1)}, u32[]{:S(2)}, u32[]{:S(2)}) %collective-permute-start.7) | collective-permute-done | bytes 163872 | tf_op jit(solution)/shard_map/ppermute | solution.py:60
  29.9 0.0 collective-permute-done.8.late
  30.0 2.4 %shard_map.58 = (f32[12,5,48,128]{3,2,1,0:T(8,128)S(1)}, f32[12,5,8,128]{3,2,1,0:T(8,128)S(1)}, f32[12,19,48,128]{3,2,1,0:T(8,128)S(1)}, f32[12,19,48,128]{3,2,1...) custom-call(f32[5,2,32,128]{3,2,1,0:T(8,128)S(1)} %collective-permut, ...), custom_call_target="tpu_custom_call", output_to_operand_aliasing={{0}: (2, {}), {1}: (3, {}), {2}: (4, {}), {3}: (5, {}), {4}... | custom-call | flops 100000000 | tf_op jit(solution)/shard_map/pallas_call | solution.py:442
  32.4 0.0 collective-permute-done.6.halo
  32.4 2.1 %shard_map.59 = (f32[4,32,128]{2,1,0:T(8,128)}, f32[3,4,32,128]{3,2,1,0:T(8,128)}, f32[12,5,48,128]{3,2,1,0:T(8,128)S(1)}, f32[12,5,8,128]{3,2,1,0:T(8,128)S(1)}...) custom-call(f32[200,128]{1,0:T(8,128)S(1)} %collective-permute-done., ...), custom_call_target="tpu_custom_call", output_to_operand_aliasing={{2}: (1, {}), {3}: (2, {}), {4}: (3, {}), {5}: (4, {}), {6}... | custom-call | flops 100000000 | tf_op jit(solution)/shard_map/pallas_call | solution.py:442
  (1 shorter events, 0.0 us)
Async XLA Ops:
  1.8 13.7 %collective-permute-start.1 = (f32[5,2,32,128]{3,2,1,0:T(8,128)S(1)}, f32[5,2,32,128]{3,2,1,0:T(8,128)S(1)}, u32[]{:S(2)}, u32[]{:S(2)}) collective-permute-start(f32[5,2,32,128]{3,2,1,0:T(8,128)S(1)} %get-tuple-element.60.early.early_own), channel_id=1, source_target_pairs={{0,16},{1,17},{2,18},{3,19},{4,20},{5,21},{6,22},{7,23},{8,24},{9,... | collective-permute-start | bytes 491528 | tf_op jit(solution)/shard_map/ppermute | solution.py:60
  5.9 9.7 %collective-permute-start.2 = (f32[5,2,32,128]{3,2,1,0:T(8,128)S(1)}, f32[5,2,32,128]{3,2,1,0:T(8,128)S(1)}, u32[]{:S(2)}, u32[]{:S(2)}) collective-permute-start(f32[5,2,32,128]{3,2,1,0:T(8,128)S(1)} %get-tuple-element.61.late.late_own), channel_id=1, source_target_pairs={{0,16},{1,17},{2,18},{3,19},{4,20},{5,21},{6,22},{7,23},{8,24},{9,... | collective-permute-start | bytes 491528 | tf_op jit(solution)/shard_map/ppermute | solution.py:60
  6.0 8.8 %collective-permute-start = (f32[40,128]{1,0:T(8,128)S(1)}, f32[40,128]{1,0:T(8,128)S(1)}, u32[]{:S(2)}, u32[]{:S(2)}) collective-permute-start(f32[40,128]{1,0:T(8,128)S(1)} %get-tuple-element.62), channel_id=1, source_target_pairs={{0,1},{1,0},{2,3},{3,2},{4,5},{5,4},{6,7},{7,6},{8,9},{9,8},{10,11... | collective-permute-start | bytes 61448 | tf_op jit(solution)/shard_map/ppermute | solution.py:60
  7.4 8.1 %collective-permute-start.3 = (f32[40,128]{1,0:T(8,128)S(1)}, f32[40,128]{1,0:T(8,128)S(1)}, u32[]{:S(2)}, u32[]{:S(2)}) collective-permute-start(f32[40,128]{1,0:T(8,128)S(1)} %get-tuple-element.62), channel_id=1, source_target_pairs={{0,17},{1,16},{2,19},{3,18},{4,21},{5,20},{6,23},{7,22},{8,25},{9,... | collective-permute-start | bytes 61448 | tf_op jit(solution)/shard_map/ppermute | solution.py:60
  15.7 8.3 %collective-permute-start.4 = (f32[184,128]{1,0:T(8,128)S(1)}, f32[184,128]{1,0:T(8,128)S(1)}, u32[]{:S(2)}, u32[]{:S(2)}) collective-permute-start(f32[184,128]{1,0:T(8,128)S(1)} %get-tuple-element.64), channel_id=1, source_target_pairs={{0,2},{1,3},{2,0},{3,1},{4,6},{5,7},{6,4},{7,5},{8,10},{9,11},{10,... | collective-permute-start | bytes 282632 | tf_op jit(solution)/shard_map/ppermute | solution.py:60
  15.7 8.2 %collective-permute-start.5 = (f32[184,128]{1,0:T(8,128)S(1)}, f32[184,128]{1,0:T(8,128)S(1)}, u32[]{:S(2)}, u32[]{:S(2)}) collective-permute-start(f32[184,128]{1,0:T(8,128)S(1)} %get-tuple-element.65), channel_id=1, source_target_pairs={{0,14},{1,15},{2,4},{3,5},{4,2},{5,3},{6,8},{7,9},{8,6},{9,7},{10,... | collective-permute-start | bytes 282632 | tf_op jit(solution)/shard_map/ppermute | solution.py:60
  18.6 11.3 %collective-permute-start.8 = (f32[360,128]{1,0:T(8,128)S(1)}, f32[360,128]{1,0:T(8,128)S(1)}, u32[]{:S(2)}, u32[]{:S(2)}) collective-permute-start(f32[360,128]{1,0:T(8,128)S(1)} %shard_map.56), channel_id=1, source_target_pairs={{0,32},{1,33},{2,34},{3,35},{4,36},{5,37},{6,38},{7,39},{8,40},{9,... | collective-permute-start | bytes 552968 | tf_op jit(solution)/shard_map/ppermute | solution.py:60
  20.3 9.7 %collective-permute-start.7 = (f32[5,2,32,128]{3,2,1,0:T(8,128)S(1)}, f32[5,2,32,128]{3,2,1,0:T(8,128)S(1)}, u32[]{:S(2)}, u32[]{:S(2)}) collective-permute-start(f32[5,2,32,128]{3,2,1,0:T(8,128)S(1)} %collective-permute-done.1.early_pair.early), channel_id=1, source_target_pairs={{0,32},{1,33},{2,34},{3,35},{4,36},{5,37},{6,38},{7,39},{8,40},{9,... | collective-permute-start | bytes 491528 | tf_op jit(solution)/shard_map/ppermute | solution.py:60
  24.1 8.3 %collective-permute-start.6 = (f32[200,128]{1,0:T(8,128)S(1)}, f32[200,128]{1,0:T(8,128)S(1)}, u32[]{:S(2)}, u32[]{:S(2)}) collective-permute-start(f32[200,128]{1,0:T(8,128)S(1)} %shard_map.55), channel_id=1, source_target_pairs={{0,32},{1,33},{2,34},{3,35},{4,36},{5,37},{6,38},{7,39},{8,40},{9,... | collective-permute-start | bytes 307208 | tf_op jit(solution)/shard_map/ppermute | solution.py:60
